TPU v7x, 32 devices: a whole 2x2x4 slice. The times are simulated.
32 devices in a mesh: fsdp: 4 (over y, x), tenant: 4 (over z), dp: 2 (over core).
Axes of the slice: x: 2, y: 2, z: 4, core: 2. Of those that a mesh axis runs over, the one named last changes fastest.
Arguments:
- tokens: bfloat16 [3072, 5120], P(('fsdp', 'dp'), 'tenant'), may hold values from -6 to 6
- block_tenant_index: int32 [48], P(('fsdp', 'dp')), may hold values from 0 to 7
- ranks: int32 [8], replicated, may hold values from 16 to 64, as said below
- frozen_up_weight: bfloat16 [5120, 14336], P(('fsdp', 'dp'), 'tenant'), may hold values from -0.078125 to 0.078125
- tenant_down_adapters: bfloat16 [8, 64, 5120], P('tenant'), may hold values from -0.078125 to 0.078125
- tenant_up_adapters: bfloat16 [8, 64, 14336], P('tenant'), may hold values from -0.75 to 0.75
- cotangent: bfloat16 [3072, 14336], P(('fsdp', 'dp'), 'tenant'), may hold values from -6 to 6
Outputs:
- hidden_out: bfloat16 [3072, 14336], P(('fsdp', 'dp'), 'tenant')
- grad_tokens: bfloat16 [3072, 5120], P(('fsdp', 'dp'), 'tenant')
- grad_down: float32 [8, 64, 5120], P('dp', None, 'tenant')
- grad_up: float32 [8, 64, 14336], P('dp', None, 'tenant')
Inputs may be any that keep to these rules, and one draw needn't show every extreme that they name: `ranks`: multiples of 16; some tenant has rank 64.
All inputs are finite; a program needn't handle non-finite values.
Results may differ from a plain program's by a relative error of at most 0.0034.
Values may be sent and summed in bfloat16 or wider, within the bound.
A program may use at most 128 MiB of HBM per device.

v0:
```python
import jax
import jax.numpy as jnp
from jax import lax
from jax.sharding import PartitionSpec as P

BLOCK = 64
alpha_scale = 32.0
BF16 = jnp.bfloat16
F32 = jnp.float32


def nt(a, b):
    return lax.dot_general(a, b, (((1,), (1,)), ((), ())), preferred_element_type=F32)


def tn(a, b):
    return lax.dot_general(a, b, (((0,), (0,)), ((), ())), preferred_element_type=F32)


def fetch_adapter(adapter, tenant_n, dp_n):
    share = adapter.shape[1] // dp_n
    mine = lax.dynamic_slice_in_dim(adapter, lax.axis_index("dp") * share, share, axis=1)
    part = lax.all_to_all(mine, "tenant", split_axis=2, concat_axis=0, tiled=True)
    return lax.all_gather(part, "dp", axis=1, tiled=True)


def reduce_fsdp(x, fsdp_n):
    rows = x.shape[0]
    got = lax.all_to_all(
        x.astype(BF16).reshape(fsdp_n, rows // fsdp_n, x.shape[1]), "fsdp", 0, 0, tiled=True
    )
    total = jnp.sum(got.astype(F32), axis=0).astype(BF16)
    return lax.all_gather(total, "fsdp", axis=0, tiled=True).astype(F32)


def make_shards(mesh):
    tenant_n, fsdp_n, dp_n = (mesh.shape["tenant"], mesh.shape["fsdp"], mesh.shape["dp"])

    def shards(
        tokens,
        block_tenant_index,
        ranks,
        frozen_up_weight,
        tenant_down_adapters,
        tenant_up_adapters,
        cotangent,
    ):
        rows, local_d = tokens.shape
        local_f = cotangent.shape[1]
        tenants = ranks.shape[0]
        rank = tenant_down_adapters.shape[1]
        depth = frozen_up_weight.shape[0]
        blocks = fsdp_n * dp_n
        first = max(128, depth * 3 // 5 // 128 * 128) if depth > 128 else depth
        cuts = [(0, first)] + ([(first, depth)] if first < depth else [])
        weights = [
            lax.all_gather(frozen_up_weight[a:b], ("fsdp", "dp"), axis=0, tiled=True)
            for a, b in cuts
        ]
        up = fetch_adapter(tenant_up_adapters, tenant_n, dp_n).reshape(tenants * rank, local_f)
        down = fetch_adapter(tenant_down_adapters, tenant_n, dp_n).reshape(tenants * rank, local_d)
        onehot = block_tenant_index[:, None] == jnp.arange(tenants, dtype=jnp.int32)[None, :]
        sel = onehot.astype(F32)[:, None, :, None]
        own_rank = jnp.sum(jnp.where(onehot, ranks[None, :], 0), axis=1)
        keep = jnp.arange(rank, dtype=jnp.int32)[None, :] < own_rank[:, None]
        gain = jnp.where(keep, (alpha_scale / own_rank.astype(F32))[:, None], F32(0.0))

        def compact(full):
            full = full.reshape(rows // BLOCK, BLOCK, tenants, rank)
            return jnp.sum(full * sel, axis=2)

        both = jnp.concatenate([compact(nt(tokens, down)), compact(nt(cotangent, up))], axis=2)
        both = lax.psum(both, "tenant")

        def spread(values):
            scaled = (values * gain[:, None, :]).astype(BF16)
            return (scaled[:, :, None, :] * sel.astype(BF16)).reshape(rows, tenants * rank)

        adapted = spread(both[:, :, :rank])
        adapted_grad = spread(both[:, :, rank:])
        terms = jnp.concatenate([tn(adapted, cotangent), tn(adapted_grad, tokens)], axis=1)
        terms = lax.psum_scatter(terms, "dp", scatter_dimension=0, tiled=True)
        grads = reduce_fsdp(terms, fsdp_n)
        grad_up = grads[:, :local_f].reshape(tenants // dp_n, rank, local_f)
        grad_down = grads[:, local_f:].reshape(tenants // dp_n, rank, local_d)
        whole = lax.all_gather(tokens, "tenant", axis=1, tiled=True)
        whole3 = whole.reshape(rows, blocks, depth)
        hidden = jnp.dot(adapted, up, preferred_element_type=F32)
        pieces = []
        for (a, b), weight in zip(cuts, weights):
            back = nt(cotangent, weight).astype(BF16)
            n = b - a
            got = lax.all_to_all(
                back.reshape(rows, tenant_n, blocks * n // tenant_n).transpose(1, 0, 2),
                "tenant",
                0,
                0,
                tiled=True,
            )
            pieces.append(jnp.sum(got.astype(F32), axis=0).reshape(rows, blocks // tenant_n, n))
            hidden = hidden + jnp.dot(
                whole3[:, :, a:b].reshape(rows, blocks * n), weight, preferred_element_type=F32
            )
        hidden_out = hidden.astype(BF16)
        grad_base = jnp.concatenate(pieces, axis=2).reshape(rows, local_d)
        grad_tokens = (grad_base + jnp.dot(adapted_grad, down, preferred_element_type=F32)).astype(
            BF16
        )
        return (hidden_out, grad_tokens, grad_down, grad_up)

    return shards


def solution(mesh):
    return jax.shard_map(
        make_shards(mesh),
        mesh=mesh,
        in_specs=(
            P(("fsdp", "dp"), "tenant"),
            P(("fsdp", "dp")),
            P(),
            P(("fsdp", "dp"), "tenant"),
            P("tenant", None, None),
            P("tenant", None, None),
            P(("fsdp", "dp"), "tenant"),
        ),
        out_specs=(
            P(("fsdp", "dp"), "tenant"),
            P(("fsdp", "dp"), "tenant"),
            P("dp", None, "tenant"),
            P("dp", None, "tenant"),
        ),
        check_vma=False,
    )
```

profile of v0, /device:TPU:0, one launch (start us, length us, event | category | flops | bytes accessed | tf_op | source)
XLA Modules:
  0.0 595.5 jit_solution(8852192433115120866)
XLA Ops:
  8.5 4.0 copy.30
  12.5 4.9 reshape.171
  17.4 6.3 %all-to-all-start = ((bf16[4,2,40960]{2,1,0:T(2,128)(2,1)}), bf16[4,2,40960]{2,1,0:T(2,128)(2,1)S(1)}, u32[]{:S(2)}, u32[]{:S(2)}) async-start(bf16[4,2,40960]{2,1,0:T(2,128)(2,1)} %reshape.171), calls=%async_computation | async-start | bytes 1310720 | tf_op jit(solution)/shard_map/all_to_all | solution.py:23
  23.8 2.8 constant_dynamic-slice_fusion
  26.6 15.2 %copy.31 = bf16[2,32,14336]{1,0,2:T(2,128)(2,1)} copy(bf16[2,32,14336]{2,1,0:T(8,128)(2,1)} %constant_dynamic-slice_fusion) | data formatting | bytes 3670016
  41.9 9.4 %reshape.173 = bf16[4,2,114688]{2,1,0:T(2,128)(2,1)} reshape(bf16[14336,2,32]{2,1,0:T(2,128)(2,1)} %bitcast.65) | data formatting | bytes 3670016
  51.3 5.1 all-to-all-start.1
  56.4 2.6 reshape.172
  59.0 6.2 %copy.28 = bf16[2,32,4,1280]{3,2,1,0:T(4,128)(2,1)S(1)} copy(bf16[2,32,4,1280]{1,0,3,2:T(2,128)(2,1)} %bitcast.70) | data formatting | bytes 1310720 | tf_op jit(solution)/shard_map/all_to_all | solution.py:23
  66.2 32.3 %all-to-all-done.1 = bf16[4,2,114688]{2,1,0:T(2,128)(2,1)} async-done(((bf16[4,2,114688]{2,1,0:T(2,128)(2,1)}), bf16[4,2,114688]{2,1,0:T(2,128)(2,1)}, u32[]{:S(2)}, u32[]{:S(2)}) %all-to-all-start.1) | async-done | bytes 1835040 | tf_op jit(solution)/shard_map/all_to_all | solution.py:23
  98.5 6.9 %reshape.174 = bf16[14336,2,32]{2,1,0:T(2,128)(2,1)} reshape(bf16[4,2,114688]{2,1,0:T(2,128)(2,1)} %all-to-all-done.1) | data formatting | bytes 3670016
  105.4 18.1 %copy.29 = bf16[2,32,4,3584]{3,2,1,0:T(4,128)(2,1)} copy(bf16[2,32,4,3584]{1,0,3,2:T(2,128)(2,1)} %bitcast.66) | data formatting | bytes 3670016 | tf_op jit(solution)/shard_map/all_to_all | solution.py:23
  123.5 3.0 copy.24
  126.7 3.3 convolution_bitcast_fusion.1
  132.9 5.8 all-gather.9.cloned.1.call-done
  138.7 5.0 convolution_bitcast_fusion
  146.6 2.9 multiply_reduce_fusion.1
  151.4 35.2 %all-reduce.2.cloned.1.call-done = f32[6,64,128]{2,1,0:T(8,128)} async-done(((f32[6,64,128]{2,1,0:T(8,128)}), f32[6,64,128]{2,1,0:T(8,128)}) %all-reduce.2.cloned.1.call-update) | async-done | bytes 196624 | tf_op jit(solution)/shard_map/psum | solution.py:73
  189.2 1.7 mul.91
  190.9 1.8 mul.87
  192.7 3.6 fusion.11
  196.3 5.0 fusion.10
  201.3 8.3 %pad_maximum_fusion = f32[512,4864]{1,0:T(8,128)} fusion(f32[512,1280]{1,0:T(8,128)} %fusion.11, f32[512,3584]{1,0:T(8,128)} %fusion.10), kind=kLoop, calls=%fused_computation | loop fusion | flops 2490368 | bytes 19922944 | tf_op jit(solution)/shard_map/concatenate | solution.py:81
  209.7 2.9 slice.28
  212.6 3.5 slice.26
  216.2 48.0 %all-gather.11.cloned.1.call-done = bf16[384,5120]{1,0:T(8,128)(2,1)} async-done(((bf16[384,1280]{1,0:T(8,128)(2,1)}), bf16[384,5120]{1,0:T(8,128)(2,1)}) %all-gather.11.cloned.1.call-update) | async-done | bytes 3932176 | tf_op jit(solution)/shard_map/all_gather | solution.py:86
  264.2 2.9 copy.34
  267.5 1.9 copy.35
  271.1 11.4 %reduce-scatter.2.cloned.1.call-done = f32[256,4864]{1,0:T(8,128)} async-done(((f32[512,4864]{1,0:T(8,128)}), f32[256,4864]{1,0:T(8,128)}) %reduce-scatter.2.cloned.1.call-update) | async-done | bytes 4980752 | tf_op jit(solution)/shard_map/reduce_scatter | solution.py:82
  282.5 4.1 convert_element_type.69
  286.6 4.6 all-to-all-start.4
  291.2 6.6 %fusion.8 = f32[384,3584]{1,0:T(8,128)} fusion(bf16[384,512]{1,0:T(8,128)(2,1)S(1)} %mul.87, bf16[512,3584]{1,0:T(8,128)(2,1)} %bitcast.82), kind=kOutput, calls=%fused_computation.33 | convolution fusion | flops 1409286144 | bytes 9568256 | tf_op jit(solution)/shard_map/dot_general | solution.py:88
  297.8 92.3 %all-gather.15.cloned.1.call-done = bf16[2048,3584]{1,0:T(8,128)(2,1)} async-done(((bf16[256,3584]{1,0:T(8,128)(2,1)}), bf16[2048,3584]{1,0:T(8,128)(2,1)}) %all-gather.15.cloned.1.call-update) | async-done | bytes 14680080 | tf_op jit(solution)/shard_map/all_gather | solution.py:57
  390.1 9.4 %convolution_convert_fusion.1 = bf16[384,2048]{1,0:T(8,128)(2,1)S(1)} fusion(bf16[384,3584]{1,0:T(8,128)(2,1)S(1)} %copy-done, bf16[2048,3584]{1,0:T(8,128)(2,1)} %all-gather.15.cloned.1.call-done), kind=kOutput, calls=%fused_computation.9 | convolution fusion | flops 5637931008 | bytes 19005440 | tf_op jit(solution)/shard_map/dot_general | solution.py:13
  400.9 4.6 all-to-all-start.3
  405.5 3.1 reduce_sum.62
  408.6 95.9 %all-gather.13.cloned.1.call-done = bf16[3072,3584]{1,0:T(8,128)(2,1)} async-done(((bf16[384,3584]{1,0:T(8,128)(2,1)}), bf16[3072,3584]{1,0:T(8,128)(2,1)}) %all-gather.13.cloned.1.call-update) | async-done | bytes 22020112 | tf_op jit(solution)/shard_map/all_gather | solution.py:57
  504.5 14.0 %convolution_convert_fusion = bf16[384,3072]{1,0:T(8,128)(2,1)} fusion(bf16[384,3584]{1,0:T(8,128)(2,1)S(1)} %copy-done, bf16[3072,3584]{1,0:T(8,128)(2,1)} %all-gather.13.cloned.1.call-done), kind=kOutput, calls=%fused_computation.5 | convolution fusion | flops 8456896512 | bytes 27131904 | tf_op jit(solution)/shard_map/dot_general | solution.py:13
  518.6 3.2 copy.40
  521.8 4.7 all-to-all-start.2
  526.5 11.6 %fusion.9 = f32[384,3584]{1,0:T(8,128)} fusion(bf16[384,2048]{1,0:T(8,128)(2,1)S(1)} %bitcast.87, bf16[2048,3584]{1,0:T(8,128)(2,1)} %all-gather.15.cloned.1.call-done), kind=kOutput, calls=%fused_computation.34 | convolution fusion | flops 5637144576 | bytes 21757952 | tf_op jit(solution)/shard_map/dot_general | solution.py:101
  541.2 4.2 all-gather.17.cloned.1.call-done
  545.4 2.4 slice.36
  547.8 2.3 slice.37
  550.1 18.7 %fusion.1 = bf16[384,3584]{1,0:T(8,128)(2,1)} fusion(f32[384,3584]{1,0:T(8,128)} %fusion.9, f32[384,3584]{1,0:T(8,128)} %fusion.8, bf16[384,3072]{1,0:T(8,128)(2,1)S(1)} %bitcast.85, bf16[3072,3584]{1,0:T(8,128)(2,1)} %all-gather.13.cloned.1.call-done), kind=kOutput, calls=%fused_computation.3 | convolution fusion | flops 8459845632 | bytes 38141952 | tf_op jit(solution)/shard_map/dot_general | solution.py:101
  568.8 12.2 %all-to-all-done.2 = bf16[4,384,768]{2,1,0:T(8,128)(2,1)} async-done(((bf16[4,384,768]{2,1,0:T(8,128)(2,1)}), bf16[4,384,768]{2,1,0:T(8,128)(2,1)}, u32[]{:S(2)}, u32[]{:S(2)}) %all-to-all-start.2) | async-done | bytes 2359328 | tf_op jit(solution)/shard_map/all_to_all | solution.py:93
  581.0 2.1 convert_reduce_fusion
  583.8 2.0 pad_maximum_fusion.1
  (58 shorter events, 22.7 us)
Async XLA Ops:
  7.2 131.6 %copy-start = (bf16[384,3584]{1,0:T(8,128)(2,1)S(1)}, bf16[384,3584]{1,0:T(8,128)(2,1)}, u32[]{:S(2)}) copy-start(bf16[384,3584]{1,0:T(8,128)(2,1)} %param.13) | copy-start | bytes 8257540
  17.4 33.8 %all-to-all-start = ((bf16[4,2,40960]{2,1,0:T(2,128)(2,1)}), bf16[4,2,40960]{2,1,0:T(2,128)(2,1)S(1)}, u32[]{:S(2)}, u32[]{:S(2)}) async-start(bf16[4,2,40960]{2,1,0:T(2,128)(2,1)} %reshape.171), calls=%async_computation | async-start | bytes 1310720 | tf_op jit(solution)/shard_map/all_to_all | solution.py:23
  51.3 47.2 %all-to-all-start.1 = ((bf16[4,2,114688]{2,1,0:T(2,128)(2,1)}), bf16[4,2,114688]{2,1,0:T(2,128)(2,1)}, u32[]{:S(2)}, u32[]{:S(2)}) async-start(bf16[4,2,114688]{2,1,0:T(2,128)(2,1)} %reshape.173), calls=%async_computation.1 | async-start | bytes 3670016 | tf_op jit(solution)/shard_map/all_to_all | solution.py:23
  56.4 70.4 %all-gather.7.cloned.1.call-start = ((), (), s32[]{:S(2)}) async-start(), calls=%async_computation.6 | async-start | bytes 1966080 | tf_op jit(solution)/shard_map/all_gather | solution.py:24
  66.1 72.6 %all-gather.9.cloned.1.call-start = ((), (), s32[]{:S(2)}) async-start(), calls=%async_computation.7 | async-start | bytes 5505024 | tf_op jit(solution)/shard_map/all_gather | solution.py:24
  123.5 3.1 copy-start.6
  126.6 60.1 %all-reduce.2.cloned.1.call-start = ((), (), s32[]{:S(2)}) async-start(), calls=%async_computation.8 | async-start | bytes 393216 | tf_op jit(solution)/shard_map/psum | solution.py:73
  146.6 4.6 copy-start.7
  150.3 113.9 %all-gather.11.cloned.1.call-start = ((), (), s32[]{:S(2)}) async-start(), calls=%async_computation.9 | async-start | bytes 4915200 | tf_op jit(solution)/shard_map/all_gather | solution.py:86
  150.9 131.6 %reduce-scatter.2.cloned.1.call-start = ((), (), s32[]{:S(2)}) async-start(), calls=%async_computation.12 | async-start | bytes 14942208 | tf_op jit(solution)/shard_map/reduce_scatter | solution.py:82
  209.6 180.5 %all-gather.15.cloned.1.call-start = ((), (), s32[]{:S(2)}) async-start(), calls=%async_computation.11 | async-start | bytes 16515072 | tf_op jit(solution)/shard_map/all_gather | solution.py:57
  212.6 291.9 %all-gather.13.cloned.1.call-start = ((), (), s32[]{:S(2)}) async-start(), calls=%async_computation.10 | async-start | bytes 24772608 | tf_op jit(solution)/shard_map/all_gather | solution.py:57
  286.6 114.2 %all-to-all-start.4 = ((bf16[4,64,4864]{2,1,0:T(8,128)(2,1)}), bf16[4,64,4864]{2,1,0:T(8,128)(2,1)}, u32[]{:S(2)}, u32[]{:S(2)}) async-start(bf16[4,64,4864]{2,1,0:T(8,128)(2,1)} %bitcast.71), calls=%async_computation.5 | async-start | bytes 4980736 | tf_op jit(solution)/shard_map/all_to_all | solution.py:29
  400.9 120.9 %all-to-all-start.3 = ((bf16[4,384,512]{2,1,0:T(8,128)(2,1)}), bf16[4,384,512]{2,1,0:T(8,128)(2,1)}, u32[]{:S(2)}, u32[]{:S(2)}) async-start(bf16[4,384,512]{2,1,0:T(8,128)(2,1)} %bitcast.77), calls=%async_computation.3 | async-start | bytes 3145728 | tf_op jit(solution)/shard_map/all_to_all | solution.py:93
  405.5 139.9 %all-gather.17.cloned.1.call-start = ((), (), s32[]{:S(2)}) async-start(), calls=%async_computation.13 | async-start | bytes 3112960 | tf_op jit(solution)/shard_map/all_gather | solution.py:33
  521.8 4.7 copy-start.4
  521.8 59.2 %all-to-all-start.2 = ((bf16[4,384,768]{2,1,0:T(8,128)(2,1)}), bf16[4,384,768]{2,1,0:T(8,128)(2,1)}, u32[]{:S(2)}, u32[]{:S(2)}) async-start(bf16[4,384,768]{2,1,0:T(8,128)(2,1)} %bitcast.62), calls=%async_computation.2 | async-start | bytes 4718592 | tf_op jit(solution)/shard_map/all_to_all | solution.py:93
  545.4 2.4 copy-start.2
  547.8 2.3 copy-start.3
  585.8 1.3 copy-start.5
  585.8 2.9 copy-start.1
Sparse Core Ops, SparseCore 0:
  66.2 10.8 all-gather.6
  126.7 11.9 all-gather.8
  150.5 36.1 all-reduce.1
  188.1 76.0 all-gather.10
  266.4 16.1 reduce-scatter.1
  284.3 105.8 all-gather.14
  392.6 111.8 all-gather.12
  506.9 38.4 all-gather.16
where the time goes:
time: 598 us; the launch traced here: 596 us
  waiting for transfers between devices  338 us (57%)
  local copies, waits for them, and re-layouts  111 us (19%)
  matrix products  79 us (13%)
  other arithmetic  27.8 us (5%)
  starting transfers between devices  25.8 us (4%)
  between operations  14.3 us (2%)
    all_gather x2, waiting for transfers between devices, shards(): lax.all_gather(frozen_up_weight[a:b], ('fsdp', 'dp'), axis=0, tiled=True)  188 us
    unnamed x26, local copies, waits for them, and re-layouts  51 us
    all_gather x1, waiting for transfers between devices, shards(): whole = lax.all_gather(tokens, 'tenant', axis=1, tiled=True)  48 us
    psum x1, waiting for transfers between devices, shards(): both = lax.psum(both, 'tenant')  35.2 us
    all_to_all x2, waiting for transfers between devices, fetch_adapter(): lax.all_to_all(mine, 'tenant', split_axis=2, concat_axis=0, tiled=True)  32.3 us
    dot_general x4, matrix products, nt(): lax.dot_general(a, b, (((1,), (1,)), ((), ())), preferred_element_type=F32)  31.8 us
    dot_general x2, matrix products, shards(): jnp.dot(whole3[:, :, a:b].reshape(rows, blocks * n), weight, preferred_el...  30.3 us
    all_to_all x4, local copies, waits for them, and re-layouts, fetch_adapter(): lax.all_to_all(mine, 'tenant', split_axis=2, concat_axis=0, tiled=True)  28.3 us
  transfers between devices with their start and end apart: 13, of which 9 were waited for; matrix products, arithmetic and copies ran while one was open for 32% of the time, Pallas kernels for 0%

commit v1 on v0

--- a/solution.py
+++ b/solution.py
@@ -7,6 +7,11 @@
 alpha_scale = 32.0
 BF16 = jnp.bfloat16
 F32 = jnp.float32
+
+
+def lift_figure_by_axis(base_x):
+    r2 = jnp.sum(lax.all_gather(base_x, "tenant"), axis=0)
+    return r2
 
 
 def nt(a, b):
@@ -70,7 +75,7 @@
             return jnp.sum(full * sel, axis=2)
 
         both = jnp.concatenate([compact(nt(tokens, down)), compact(nt(cotangent, up))], axis=2)
-        both = lax.psum(both, "tenant")
+        both = lift_figure_by_axis(both)
 
         def spread(values):
             scaled = (values * gain[:, None, :]).astype(BF16)

time: 598 us -> 564 us (0.943)
  waiting for transfers between devices: 338 us -> 273 us
  blocking collectives: 0 us -> 30.7 us
    psum x1 -> x0, waiting for transfers between devices: 35.2 us -> none  [shards(): both = lax.psum(both, 'tenant')]
    all_gather x0 -> x1, blocking collectives: none -> 30.7 us  [lift_figure_by_axis(): r2 = jnp.sum(lax.all_gather(base_x, 'tenant'), axis=0)]
    all_gather x1, waiting for transfers between devices: 48 us -> 19.7 us  [shards(): whole = lax.all_gather(tokens, 'tenant', axis=1, tiled=True)]
  transfers between devices with their start and end apart: 13 -> 12, of which waited for: 9 -> 8; matrix products, arithmetic and copies ran while one was open for 32% -> 36% of each run, Pallas kernels for 0% -> 0%
where the time goes in v1:
time: 564 us; the launch traced here: 562 us
  waiting for transfers between devices  273 us (48%)
  local copies, waits for them, and re-layouts  111 us (20%)
  matrix products  79 us (14%)
  blocking collectives  30.7 us (5%)
  other arithmetic  28 us (5%)
  starting transfers between devices  25.6 us (5%)
  between operations  14.3 us (3%)
    all_gather x2, waiting for transfers between devices, shards(): lax.all_gather(frozen_up_weight[a:b], ('fsdp', 'dp'), axis=0, tiled=True)  188 us
    unnamed x26, local copies, waits for them, and re-layouts  51 us
    all_to_all x2, waiting for transfers between devices, fetch_adapter(): lax.all_to_all(mine, 'tenant', split_axis=2, concat_axis=0, tiled=True)  32.3 us
    dot_general x4, matrix products, nt(): lax.dot_general(a, b, (((1,), (1,)), ((), ())), preferred_element_type=F32)  31.9 us
    all_gather x1, blocking collectives, lift_figure_by_axis(): r2 = jnp.sum(lax.all_gather(base_x, 'tenant'), axis=0)  30.7 us
    dot_general x2, matrix products, shards(): jnp.dot(whole3[:, :, a:b].reshape(rows, blocks * n), weight, preferred_el...  30.3 us
    all_to_all x4, local copies, waits for them, and re-layouts, fetch_adapter(): lax.all_to_all(mine, 'tenant', split_axis=2, concat_axis=0, tiled=True)  28.3 us
    all_gather x1, waiting for transfers between devices, shards(): whole = lax.all_gather(tokens, 'tenant', axis=1, tiled=True)  19.7 us
  transfers between devices with their start and end apart: 12, of which 8 were waited for; matrix products, arithmetic and copies ran while one was open for 36% of the time, Pallas kernels for 0%

profile of v1, /device:TPU:0, one launch (start us, length us, event | category | flops | bytes accessed | tf_op | source)
XLA Modules:
  0.0 561.7 jit_solution(6884710989709571941)
XLA Ops:
  8.5 4.0 copy.30
  12.5 4.9 reshape.172
  17.4 6.3 %all-to-all-start = ((bf16[4,2,40960]{2,1,0:T(2,128)(2,1)}), bf16[4,2,40960]{2,1,0:T(2,128)(2,1)S(1)}, u32[]{:S(2)}, u32[]{:S(2)}) async-start(bf16[4,2,40960]{2,1,0:T(2,128)(2,1)} %reshape.172), calls=%async_computation | async-start | bytes 1310720 | tf_op jit(solution)/shard_map/all_to_all | solution.py:28
  23.8 2.8 constant_dynamic-slice_fusion
  26.6 15.2 %copy.31 = bf16[2,32,14336]{1,0,2:T(2,128)(2,1)} copy(bf16[2,32,14336]{2,1,0:T(8,128)(2,1)} %constant_dynamic-slice_fusion) | data formatting | bytes 3670016
  41.9 9.4 %reshape.174 = bf16[4,2,114688]{2,1,0:T(2,128)(2,1)} reshape(bf16[14336,2,32]{2,1,0:T(2,128)(2,1)} %bitcast.66) | data formatting | bytes 3670016
  51.3 5.1 all-to-all-start.1
  56.3 2.6 reshape.173
  59.0 6.2 %copy.28 = bf16[2,32,4,1280]{3,2,1,0:T(4,128)(2,1)S(1)} copy(bf16[2,32,4,1280]{1,0,3,2:T(2,128)(2,1)} %bitcast.71) | data formatting | bytes 1310720 | tf_op jit(solution)/shard_map/all_to_all | solution.py:28
  66.2 32.3 %all-to-all-done.1 = bf16[4,2,114688]{2,1,0:T(2,128)(2,1)} async-done(((bf16[4,2,114688]{2,1,0:T(2,128)(2,1)}), bf16[4,2,114688]{2,1,0:T(2,128)(2,1)}, u32[]{:S(2)}, u32[]{:S(2)}) %all-to-all-start.1) | async-done | bytes 1835040 | tf_op jit(solution)/shard_map/all_to_all | solution.py:28
  98.5 6.9 %reshape.175 = bf16[14336,2,32]{2,1,0:T(2,128)(2,1)} reshape(bf16[4,2,114688]{2,1,0:T(2,128)(2,1)} %all-to-all-done.1) | data formatting | bytes 3670016
  105.4 18.1 %copy.29 = bf16[2,32,4,3584]{3,2,1,0:T(4,128)(2,1)} copy(bf16[2,32,4,3584]{1,0,3,2:T(2,128)(2,1)} %bitcast.67) | data formatting | bytes 3670016 | tf_op jit(solution)/shard_map/all_to_all | solution.py:28
  123.5 3.1 copy.24
  127.7 3.3 convolution_bitcast_fusion.1
  134.0 4.8 all-gather.10.cloned.1.call-done
  138.8 5.0 convolution_bitcast_fusion
  146.6 3.1 multiply_reduce_fusion.1
  149.8 30.7 %all-gather = f32[24,64,128]{2,1,0:T(8,128)S(1)} all-gather(f32[6,64,128]{2,1,0:T(8,128)S(1)} %pad_maximum_fusion.2), channel_id=2, replica_groups=mesh['fsdp'=4,'tenant'=4,'dp'=2] {'tenant'}, dimensions={0}, use_global_device_ids=true | all-gather | bytes 983040 | tf_op jit(solution)/shard_map/all_gather | solution.py:13
  183.8 1.8 mul.91
  185.5 1.8 mul.87
  187.3 3.6 fusion.11
  190.9 5.0 fusion.10
  195.9 8.3 %pad_maximum_fusion = f32[512,4864]{1,0:T(8,128)} fusion(f32[512,1280]{1,0:T(8,128)} %fusion.11, f32[512,3584]{1,0:T(8,128)} %fusion.10), kind=kLoop, calls=%fused_computation | loop fusion | flops 2490368 | bytes 19922944 | tf_op jit(solution)/shard_map/concatenate | solution.py:86
  204.2 2.9 slice.28
  207.2 3.5 slice.26
  210.7 19.7 %all-gather.12.cloned.1.call-done = bf16[384,5120]{1,0:T(8,128)(2,1)} async-done(((bf16[384,1280]{1,0:T(8,128)(2,1)}), bf16[384,5120]{1,0:T(8,128)(2,1)}) %all-gather.12.cloned.1.call-update) | async-done | bytes 3932176 | tf_op jit(solution)/shard_map/all_gather | solution.py:91
  230.5 2.9 copy.34
  233.8 2.0 copy.35
  237.4 11.5 %reduce-scatter.2.cloned.1.call-done = f32[256,4864]{1,0:T(8,128)} async-done(((f32[512,4864]{1,0:T(8,128)}), f32[256,4864]{1,0:T(8,128)}) %reduce-scatter.2.cloned.1.call-update) | async-done | bytes 4980752 | tf_op jit(solution)/shard_map/reduce_scatter | solution.py:87
  248.8 4.1 convert_element_type.69
  253.0 4.5 all-to-all-start.4
  257.5 6.6 %fusion.8 = f32[384,3584]{1,0:T(8,128)} fusion(bf16[384,512]{1,0:T(8,128)(2,1)S(1)} %mul.87, bf16[512,3584]{1,0:T(8,128)(2,1)} %bitcast.83), kind=kOutput, calls=%fused_computation.33 | convolution fusion | flops 1409286144 | bytes 9568256 | tf_op jit(solution)/shard_map/dot_general | solution.py:93
  264.1 92.3 %all-gather.16.cloned.1.call-done = bf16[2048,3584]{1,0:T(8,128)(2,1)} async-done(((bf16[256,3584]{1,0:T(8,128)(2,1)}), bf16[2048,3584]{1,0:T(8,128)(2,1)}) %all-gather.16.cloned.1.call-update) | async-done | bytes 14680080 | tf_op jit(solution)/shard_map/all_gather | solution.py:62
  356.4 9.5 %convolution_convert_fusion.1 = bf16[384,2048]{1,0:T(8,128)(2,1)S(1)} fusion(bf16[384,3584]{1,0:T(8,128)(2,1)S(1)} %copy-done, bf16[2048,3584]{1,0:T(8,128)(2,1)} %all-gather.16.cloned.1.call-done), kind=kOutput, calls=%fused_computation.9 | convolution fusion | flops 5637931008 | bytes 19005440 | tf_op jit(solution)/shard_map/dot_general | solution.py:18
  367.2 4.6 all-to-all-start.3
  371.9 3.1 reduce_sum.72
  375.0 95.7 %all-gather.14.cloned.1.call-done = bf16[3072,3584]{1,0:T(8,128)(2,1)} async-done(((bf16[384,3584]{1,0:T(8,128)(2,1)}), bf16[3072,3584]{1,0:T(8,128)(2,1)}) %all-gather.14.cloned.1.call-update) | async-done | bytes 22020112 | tf_op jit(solution)/shard_map/all_gather | solution.py:62
  470.6 14.1 %convolution_convert_fusion = bf16[384,3072]{1,0:T(8,128)(2,1)} fusion(bf16[384,3584]{1,0:T(8,128)(2,1)S(1)} %copy-done, bf16[3072,3584]{1,0:T(8,128)(2,1)} %all-gather.14.cloned.1.call-done), kind=kOutput, calls=%fused_computation.5 | convolution fusion | flops 8456896512 | bytes 27131904 | tf_op jit(solution)/shard_map/dot_general | solution.py:18
  484.7 3.2 copy.40
  487.9 4.7 all-to-all-start.2
  492.6 11.6 %fusion.9 = f32[384,3584]{1,0:T(8,128)} fusion(bf16[384,2048]{1,0:T(8,128)(2,1)S(1)} %bitcast.89, bf16[2048,3584]{1,0:T(8,128)(2,1)} %all-gather.16.cloned.1.call-done), kind=kOutput, calls=%fused_computation.34 | convolution fusion | flops 5637144576 | bytes 21757952 | tf_op jit(solution)/shard_map/dot_general | solution.py:106
  507.3 4.2 all-gather.18.cloned.1.call-done
  511.5 2.4 slice.36
  513.9 2.3 slice.37
  516.2 18.7 %fusion.1 = bf16[384,3584]{1,0:T(8,128)(2,1)} fusion(f32[384,3584]{1,0:T(8,128)} %fusion.9, f32[384,3584]{1,0:T(8,128)} %fusion.8, bf16[384,3072]{1,0:T(8,128)(2,1)S(1)} %bitcast.87, bf16[3072,3584]{1,0:T(8,128)(2,1)} %all-gather.14.cloned.1.call-done), kind=kOutput, calls=%fused_computation.3 | convolution fusion | flops 8459845632 | bytes 38141952 | tf_op jit(solution)/shard_map/dot_general | solution.py:106
  535.0 12.2 %all-to-all-done.2 = bf16[4,384,768]{2,1,0:T(8,128)(2,1)} async-done(((bf16[4,384,768]{2,1,0:T(8,128)(2,1)}), bf16[4,384,768]{2,1,0:T(8,128)(2,1)}, u32[]{:S(2)}, u32[]{:S(2)}) %all-to-all-start.2) | async-done | bytes 2359328 | tf_op jit(solution)/shard_map/all_to_all | solution.py:98
  547.2 2.1 convert_reduce_fusion
  549.9 2.0 pad_maximum_fusion.1
  (57 shorter events, 22.7 us)
Async XLA Ops:
  7.2 131.6 %copy-start = (bf16[384,3584]{1,0:T(8,128)(2,1)S(1)}, bf16[384,3584]{1,0:T(8,128)(2,1)}, u32[]{:S(2)}) copy-start(bf16[384,3584]{1,0:T(8,128)(2,1)} %param.13) | copy-start | bytes 8257540
  17.4 33.8 %all-to-all-start = ((bf16[4,2,40960]{2,1,0:T(2,128)(2,1)}), bf16[4,2,40960]{2,1,0:T(2,128)(2,1)S(1)}, u32[]{:S(2)}, u32[]{:S(2)}) async-start(bf16[4,2,40960]{2,1,0:T(2,128)(2,1)} %reshape.172), calls=%async_computation | async-start | bytes 1310720 | tf_op jit(solution)/shard_map/all_to_all | solution.py:28
  51.3 47.2 %all-to-all-start.1 = ((bf16[4,2,114688]{2,1,0:T(2,128)(2,1)}), bf16[4,2,114688]{2,1,0:T(2,128)(2,1)}, u32[]{:S(2)}, u32[]{:S(2)}) async-start(bf16[4,2,114688]{2,1,0:T(2,128)(2,1)} %reshape.174), calls=%async_computation.1 | async-start | bytes 3670016 | tf_op jit(solution)/shard_map/all_to_all | solution.py:28
  56.3 71.4 %all-gather.8.cloned.1.call-start = ((), (), s32[]{:S(2)}) async-start(), calls=%async_computation.6 | async-start | bytes 1966080 | tf_op jit(solution)/shard_map/all_gather | solution.py:29
  66.1 72.7 %all-gather.10.cloned.1.call-start = ((), (), s32[]{:S(2)}) async-start(), calls=%async_computation.7 | async-start | bytes 5505024 | tf_op jit(solution)/shard_map/all_gather | solution.py:29
  123.5 3.9 copy-start.6
  123.5 3.9 copy-start.7
  126.6 103.9 %all-gather.12.cloned.1.call-start = ((), (), s32[]{:S(2)}) async-start(), calls=%async_computation.8 | async-start | bytes 4915200 | tf_op jit(solution)/shard_map/all_gather | solution.py:91
  127.3 121.5 %reduce-scatter.2.cloned.1.call-start = ((), (), s32[]{:S(2)}) async-start(), calls=%async_computation.11 | async-start | bytes 14942208 | tf_op jit(solution)/shard_map/reduce_scatter | solution.py:87
  204.2 152.2 %all-gather.16.cloned.1.call-start = ((), (), s32[]{:S(2)}) async-start(), calls=%async_computation.10 | async-start | bytes 16515072 | tf_op jit(solution)/shard_map/all_gather | solution.py:62
  207.2 263.5 %all-gather.14.cloned.1.call-start = ((), (), s32[]{:S(2)}) async-start(), calls=%async_computation.9 | async-start | bytes 24772608 | tf_op jit(solution)/shard_map/all_gather | solution.py:62
  253.0 114.2 %all-to-all-start.4 = ((bf16[4,64,4864]{2,1,0:T(8,128)(2,1)}), bf16[4,64,4864]{2,1,0:T(8,128)(2,1)}, u32[]{:S(2)}, u32[]{:S(2)}) async-start(bf16[4,64,4864]{2,1,0:T(8,128)(2,1)} %bitcast.72), calls=%async_computation.5 | async-start | bytes 4980736 | tf_op jit(solution)/shard_map/all_to_all | solution.py:34
  367.2 120.7 %all-to-all-start.3 = ((bf16[4,384,512]{2,1,0:T(8,128)(2,1)}), bf16[4,384,512]{2,1,0:T(8,128)(2,1)}, u32[]{:S(2)}, u32[]{:S(2)}) async-start(bf16[4,384,512]{2,1,0:T(8,128)(2,1)} %bitcast.78), calls=%async_computation.3 | async-start | bytes 3145728 | tf_op jit(solution)/shard_map/all_to_all | solution.py:98
  371.8 139.7 %all-gather.18.cloned.1.call-start = ((), (), s32[]{:S(2)}) async-start(), calls=%async_computation.12 | async-start | bytes 3112960 | tf_op jit(solution)/shard_map/all_gather | solution.py:38
  487.9 4.7 copy-start.4
  487.9 59.2 %all-to-all-start.2 = ((bf16[4,384,768]{2,1,0:T(8,128)(2,1)}), bf16[4,384,768]{2,1,0:T(8,128)(2,1)}, u32[]{:S(2)}, u32[]{:S(2)}) async-start(bf16[4,384,768]{2,1,0:T(8,128)(2,1)} %bitcast.63), calls=%async_computation.2 | async-start | bytes 4718592 | tf_op jit(solution)/shard_map/all_to_all | solution.py:98
  511.5 2.4 copy-start.2
  513.9 2.3 copy-start.3
  551.9 1.3 copy-start.5
  551.9 2.9 copy-start.1
Sparse Core Ops, SparseCore 0:
  66.2 10.8 all-gather.7
  126.7 12.0 all-gather.9
  140.3 90.0 all-gather.11
  232.6 16.1 reduce-scatter.1
  250.6 105.7 all-gather.15
  358.7 111.8 all-gather.13
  473.1 38.4 all-gather.17
